TPU v7x, 8 devices: a whole 2x2x1 slice. The times are simulated.
8 devices in a mesh: fit: 1 (over z), comp: 2 (over y), pts: 4 (over x, core).
Axes of the slice: x: 2, y: 2, z: 1, core: 2. Of those that a mesh axis runs over, the one named last changes fastest.
Arguments:
- points: bfloat16 [2048, 128], P(('fit', 'pts'))
- means_init: float32 [65536, 128], P(('fit', 'comp'))
- logw_init: float32 [65536], P(('fit', 'comp'))
- inv_temp: float32 [3], replicated
Outputs:
- output 1: float32 [65536, 128], P(('fit', 'comp'))
- output 2: float32 [65536], P(('fit', 'comp'))
- output 3: float32 [2048], P(('fit', 'pts'))
All inputs are finite; a program needn't handle non-finite values.
Results may differ from a plain program's by a relative error of at most 0.001.
Values are sent between devices in bfloat16 or wider.
A program may use at most 1 GiB of HBM per device.

v0:
```python
import jax
import jax.numpy as jnp
from jax import lax
from jax.sharding import PartitionSpec as P

PRIOR_ALPHA = 1e-3
COUNT_EPS = 1e-6


def solution(mesh):
    row_groups = mesh.shape["pts"]
    comp_groups = mesh.shape["comp"]

    def per_device(points, mean_vecs, log_w, inv_temp):
        n_total = points.shape[0] * row_groups
        k_total = mean_vecs.shape[0] * comp_groups
        x_sq = jnp.einsum("nd,nd->n", points, points, preferred_element_type=jnp.float32)
        log_norm = None
        for sweep_idx in range(inv_temp.shape[0]):
            mean_bf = mean_vecs.astype(jnp.bfloat16)
            mean_sq = jnp.sum(mean_vecs * mean_vecs, axis=1)
            cross_dot = jnp.einsum("nd,kd->nk", points, mean_bf, preferred_element_type=jnp.float32)
            logits = log_w[None, :] - inv_temp[sweep_idx] * (x_sq[:, None] - 2.0 * cross_dot + mean_sq[None, :])
            row_top = lax.pmax(jnp.max(logits, axis=1), "comp")
            exp_total = lax.psum(jnp.sum(jnp.exp(logits - row_top[:, None]), axis=1), "comp")
            log_norm = row_top + jnp.log(exp_total)
            resp_prob = jnp.exp(logits - log_norm[:, None])
            counts = jnp.sum(resp_prob, axis=0)
            stat_sums = jnp.einsum("nk,nd->kd", resp_prob.astype(jnp.bfloat16), points, preferred_element_type=jnp.float32)
            counts, stat_sums = lax.psum((counts, stat_sums), "pts")
            mean_vecs = stat_sums / (counts[:, None] + COUNT_EPS)
            log_w = jnp.log((counts + PRIOR_ALPHA) / (n_total + k_total * PRIOR_ALPHA))
        return mean_vecs, log_w, log_norm

    row_spec = P(("fit", "pts"))
    comp_spec = P(("fit", "comp"))
    return jax.shard_map(
        per_device,
        mesh=mesh,
        in_specs=(P(("fit", "pts"), None), P(("fit", "comp"), None), comp_spec, P()),
        out_specs=(P(("fit", "comp"), None), comp_spec, row_spec),
        check_vma=False,
    )
```

profile of v0, /device:TPU:0, one launch (start us, length us, event | category | flops | bytes accessed | tf_op | source)
XLA Modules:
  0.0 1279.8 jit_solution(7550916949210107176)
XLA Ops:
  7.2 0.0 all-reduce.11.cloned.1.call-start
  7.2 1.4 fusion.19
  8.6 1.0 fusion.18
  9.7 8.2 multiply_reduce_fusion.2
  17.9 31.6 %fusion.20 = (f32[512]{0:T(512)S(1)}, f32[512,32768]{1,0:T(8,128)}) fusion(f32[32768]{0:T(1024)S(1)} %multiply_reduce_fusion.2, bf16[512,128]{1,0:T(8,128)(2,1)} %param.4, f32[32768,128]{1,0:T(8,128)} %param.5, f32[512]{0:T(512)S(1)} %fusion.18, f32[]{:T(128)} %bitcast, f32[32768]{0:T(1024)} %param.6), kind=kOutput, calls=%fused_computation.42 | convolution fusion | flops 4399824384 | bytes 84283392 | tf_op jit(solution)/shard_map/nd,kd->nk/dot_general | solution.py:22
  49.5 6.2 pmax.21
  55.8 0.0 copy-start
  55.8 21.2 %exponential_reduce_fusion.2 = f32[512]{0:T(512)S(1)} fusion(f32[512,32768]{1,0:T(8,128)} %get-tuple-element.19, f32[512]{0:T(512)S(1)} %pmax.21), kind=kLoop, calls=%fused_computation.7 | loop fusion | flops 33553920 | bytes 67112960 | tf_op jit(solution)/shard_map/reduce_sum | solution.py:25
  76.9 4.9 psum.63
  81.9 22.0 %fusion.1 = f32[32768]{0:T(1024)} fusion(f32[512,32768]{1,0:T(8,128)} %get-tuple-element.19, f32[512]{0:T(512)S(1)} %log_add_fusion.2), kind=kLoop, calls=%fused_computation.10 | loop fusion | flops 33521664 | bytes 67241984 | tf_op jit(solution)/shard_map/reduce_sum | solution.py:28
  103.8 0.0 copy-done
  103.8 29.7 %fusion.10 = f32[32768,128]{1,0:T(8,128)} fusion(bf16[512,128]{1,0:T(8,128)(2,1)S(1)} %copy-done, f32[512,32768]{1,0:T(8,128)} %get-tuple-element.19, f32[512]{0:T(512)S(1)} %log_add_fusion.2), kind=kOutput, calls=%fused_computation.17 | convolution fusion | flops 4328521728 | bytes 84019200 | tf_op jit(solution)/shard_map/nk,nd->kd/dot_general | solution.py:29
  133.5 0.0 all-reduce.11.cloned.1.call-update
  133.5 0.2 all-reduce.9.cloned.1.call-start
  133.8 285.7 %all-reduce.11.cloned.1.call-done = (f32[32768]{0:T(1024)}, f32[32768,128]{1,0:T(8,128)}) async-done(((f32[32768]{0:T(1024)}, f32[32768,128]{1,0:T(8,128)}), (f32[32768]{0:T(1024)}, f32[32768,128]{1,0:T(8,128)})) %all-reduce.11.cloned.1.call-update) | async-done | bytes 16908304 | tf_op jit(solution)/shard_map/psum | solution.py:30
  419.5 0.9 broadcast_add_fusion.2
  420.4 11.1 multiply_reduce_fusion.1
  431.5 37.6 %fusion.21 = (f32[512]{0:T(512)S(1)}, f32[32768,512]{1,0:T(8,128)}) fusion(f32[32768]{0:T(1024)S(1)} %multiply_reduce_fusion.1, bf16[512,128]{1,0:T(8,128)(2,1)S(1)} %copy-done, f32[32768,128]{1,0:T(8,128)} %get-tuple-element.8, f32[32768]{0:T(1024)S(1)} %get-tuple-element.13, f32[512]{0:T(512)S(1)} %fusion.18, f32[]{:T(128)} %bitcast.1, ...), kind=kOutput, calls=%fused_computation.43 | convolution fusion | flops 4404018688 | bytes 84414464 | tf_op jit(solution)/shard_map/nd,kd->nk/dot_general | solution.py:22
  469.1 4.9 pmax.22
  474.0 21.7 %exponential_reduce_fusion.1 = f32[512]{0:T(512)S(1)} fusion(f32[32768,512]{1,0:T(8,128)} %get-tuple-element.21, f32[512]{0:T(512)S(1)} %pmax.22), kind=kLoop, calls=%fused_computation.1 | loop fusion | flops 33553920 | bytes 67112960 | tf_op jit(solution)/shard_map/reduce_sum | solution.py:25
  495.8 4.9 psum.66
  500.7 22.5 %fusion.2 = f32[32768]{0:T(1024)} fusion(f32[32768,512]{1,0:T(8,128)} %get-tuple-element.21, f32[512]{0:T(512)S(1)} %log_add_fusion.1), kind=kLoop, calls=%fused_computation.11 | loop fusion | flops 33521664 | bytes 67241984 | tf_op jit(solution)/shard_map/reduce_sum | solution.py:28
  523.2 29.3 %fusion.8 = f32[32768,128]{1,0:T(8,128)} fusion(bf16[512,128]{1,0:T(8,128)(2,1)S(1)} %copy-done, f32[32768,512]{1,0:T(8,128)} %get-tuple-element.21, f32[512]{0:T(512)S(1)} %log_add_fusion.1), kind=kOutput, calls=%fused_computation.16 | convolution fusion | flops 4328521728 | bytes 84019200 | tf_op jit(solution)/shard_map/nk,nd->kd/dot_general | solution.py:29
  552.5 0.0 all-reduce.9.cloned.1.call-update
  552.5 0.0 all-reduce.7.cloned.1.call-start
  552.5 284.6 %all-reduce.9.cloned.1.call-done = (f32[32768]{0:T(1024)}, f32[32768,128]{1,0:T(8,128)}) async-done(((f32[32768]{0:T(1024)}, f32[32768,128]{1,0:T(8,128)}), (f32[32768]{0:T(1024)}, f32[32768,128]{1,0:T(8,128)})) %all-reduce.9.cloned.1.call-update) | async-done | bytes 16908304 | tf_op jit(solution)/shard_map/psum | solution.py:30
  837.2 0.9 broadcast_add_fusion.1
  838.1 11.1 multiply_reduce_fusion
  849.2 37.6 %fusion.22 = (f32[512]{0:T(512)S(1)}, f32[32768,512]{1,0:T(8,128)}) fusion(f32[32768]{0:T(1024)S(1)} %multiply_reduce_fusion, bf16[512,128]{1,0:T(8,128)(2,1)S(1)} %copy-done, f32[32768,128]{1,0:T(8,128)} %get-tuple-element.6, f32[32768]{0:T(1024)S(1)} %get-tuple-element.11, f32[512]{0:T(512)S(1)} %fusion.18, f32[]{:T(128)} %bitcast.2, ...), kind=kOutput, calls=%fused_computation.44 | convolution fusion | flops 4404018688 | bytes 84414464 | tf_op jit(solution)/shard_map/nd,kd->nk/dot_general | solution.py:22
  886.8 4.9 pmax.23
  891.7 21.7 %exponential_reduce_fusion = f32[512]{0:T(512)S(1)} fusion(f32[32768,512]{1,0:T(8,128)} %get-tuple-element.23, f32[512]{0:T(512)S(1)} %pmax.23), kind=kLoop, calls=%fused_computation | loop fusion | flops 33553920 | bytes 67112960 | tf_op jit(solution)/shard_map/reduce_sum | solution.py:25
  913.4 5.1 psum.69
  918.6 0.0 copy-start.1
  918.6 22.5 %fusion.4 = f32[32768]{0:T(1024)} fusion(f32[32768,512]{1,0:T(8,128)} %get-tuple-element.23, f32[512]{0:T(512)S(1)} %log_add_fusion), kind=kLoop, calls=%fused_computation.13 | loop fusion | flops 33521664 | bytes 67241984 | tf_op jit(solution)/shard_map/reduce_sum | solution.py:28
  941.1 29.3 %fusion.6 = f32[32768,128]{1,0:T(8,128)} fusion(bf16[512,128]{1,0:T(8,128)(2,1)S(1)} %copy-done, f32[32768,512]{1,0:T(8,128)} %get-tuple-element.23, f32[512]{0:T(512)S(1)} %log_add_fusion), kind=kOutput, calls=%fused_computation.15 | convolution fusion | flops 4328521728 | bytes 84019200 | tf_op jit(solution)/shard_map/nk,nd->kd/dot_general | solution.py:29
  970.3 0.0 copy-done.1
  970.3 0.0 all-reduce.7.cloned.1.call-update
  970.4 284.7 %all-reduce.7.cloned.1.call-done = (f32[32768,128]{1,0:T(8,128)}, f32[32768]{0:T(1024)}) async-done(((f32[32768,128]{1,0:T(8,128)}, f32[32768]{0:T(1024)}), (f32[32768,128]{1,0:T(8,128)}, f32[32768]{0:T(1024)})) %all-reduce.7.cloned.1.call-update) | async-done | bytes 16908304 | tf_op jit(solution)/shard_map/psum | solution.py:30
  1255.0 1.6 multiply_log_fusion
  1256.6 16.6 %broadcast_divide_fusion = f32[32768,128]{1,0:T(8,128)} fusion(f32[32768,128]{1,0:T(8,128)} %get-tuple-element.3, f32[32768]{0:T(1024)S(1)} %get-tuple-element.10), kind=kLoop, calls=%fused_computation.24 | loop fusion | flops 4194304 | bytes 33685504 | tf_op jit(solution)/shard_map/div | solution.py:31
  (3 shorter events, 0.0 us)
Async XLA Ops:
  7.2 412.3 %all-reduce.11.cloned.1.call-start = ((), (), s32[]{:S(2)}) async-start(), calls=%async_computation.2 | async-start | bytes 33816576 | tf_op jit(solution)/shard_map/psum | solution.py:30
  55.8 48.1 %copy-start = (bf16[512,128]{1,0:T(8,128)(2,1)S(1)}, bf16[512,128]{1,0:T(8,128)(2,1)}, u32[]{:S(2)}) copy-start(bf16[512,128]{1,0:T(8,128)(2,1)} %param.4) | copy-start | bytes 393220
  133.5 703.6 %all-reduce.9.cloned.1.call-start = ((), (), s32[]{:S(2)}) async-start(), calls=%async_computation.1 | async-start | bytes 33816576 | tf_op jit(solution)/shard_map/psum | solution.py:30
  552.5 702.6 %all-reduce.7.cloned.1.call-start = ((), (), s32[]{:S(2)}) async-start(), calls=%async_computation | async-start | bytes 33816576 | tf_op jit(solution)/shard_map/psum | solution.py:30
  918.6 51.8 %copy-start.1 = (f32[512]{0:T(512)}, f32[512]{0:T(512)S(1)}, u32[]{:S(2)}) copy-start(f32[512]{0:T(512)S(1)} %log_add_fusion) | copy-start | bytes 6148
Sparse Core Ops, SparseCore 0:
  133.7 285.7 all-reduce.10
  552.6 284.5 all-reduce.8
  970.5 284.5 all-reduce.6
where the time goes:
time: 1280 us
  waiting for transfers between devices  855 us (67%)
  matrix products  195 us (15%)
  other arithmetic  183 us (14%)
  blocking collectives  31.1 us (2%)
  between operations  13.8 us (1%)
    psum x3, waiting for transfers between devices, per_device(): counts, stat_sums = lax.psum((counts, stat_sums), 'pts')  855 us
    dot_general x3, matrix products, per_device(): jnp.einsum('nd,kd->nk', points, mean_bf, preferred_element_type=jnp.float32)  107 us
    dot_general x3, matrix products, per_device(): jnp.einsum('nk,nd->kd', resp_prob.astype(jnp.bfloat16), points, preferred...  88.2 us
    reduce_sum x3, other arithmetic, per_device(): counts = jnp.sum(resp_prob, axis=0)  66.9 us
    reduce_sum x3, other arithmetic, per_device(): jnp.sum(jnp.exp(logits - row_top[:, None]), axis=1)  64.6 us
    reduce_sum x3, other arithmetic, per_device(): mean_sq = jnp.sum(mean_vecs * mean_vecs, axis=1)  30.4 us
  transfers between devices with their start and end apart: 3, of which 3 were waited for; matrix products, arithmetic and copies ran while one was open for 0% of the time, Pallas kernels for 0%

commit v1 on v0

v1 whole, which is shorter than its diff:
```python
import jax
import jax.numpy as jnp
from jax import lax
from jax.experimental import pallas as pl
from jax.experimental.pallas import tpu as pltpu
from jax.sharding import PartitionSpec as P

PRIOR_ALPHA = 1e-3
COUNT_EPS = 1e-6
LOG2E = 1.4426950408889634
LN2 = 0.6931471805599453
F32 = jnp.float32
BF16 = jnp.bfloat16
D = 128
KB = 1024
IT = 256
SUB = 64
VMEM = 60 * 2**20


def split3(v):
    hi = v.astype(BF16).astype(F32)
    mid = (v - hi).astype(BF16).astype(F32)
    return hi, mid, v - hi - mid


def lane_to_col(rows):
    r = rows.shape[0]
    eye = lax.broadcasted_iota(jnp.int32, (1, D, D), 1) == lax.broadcasted_iota(jnp.int32, (1, D, D), 2)
    col = jnp.sum(jnp.where(eye, rows[:, None, :], 0.0), axis=2, keepdims=True)
    return jnp.broadcast_to(col, (r, D, D)).reshape(r * D, D)


def col_to_lane(col):
    r = col.shape[0] // D
    eye = lax.broadcasted_iota(jnp.int32, (1, D, D), 1) == lax.broadcasted_iota(jnp.int32, (1, D, D), 2)
    return jnp.sum(jnp.where(eye, jnp.broadcast_to(col, (r * D, D)).reshape(r, D, D), 0.0), axis=1)


def aug_cols(c):
    lane = lax.broadcasted_iota(jnp.int32, c.shape, 1)
    hi, mid, lo = split3(c)
    v = jnp.where(lane == 0, hi, jnp.where(lane == 1, mid, lo))
    v = jnp.where(lane < 3, v, jnp.where(lane < 6, 1.0, 0.0))
    return v.astype(BF16)


def aug_rows(t):
    row = lax.broadcasted_iota(jnp.int32, (D, t.shape[1]), 0)
    hi, mid, lo = split3(-t)
    v = jnp.where(row == 3, hi, jnp.where(row == 4, mid, lo))
    v = jnp.where(row < 3, 1.0, jnp.where(row < 6, v, 0.0))
    return v.astype(BF16)


def fill_rhs(rhs_ref, xt_ref, g, t):
    rhs_ref[0:D, :] = (xt_ref[...].astype(F32) * g).astype(BF16)
    rhs_ref[D:, :] = aug_rows(t)


def e_block(lhs, rhs_ref, k1, m_ref, s_ref):
    n = rhs_ref.shape[1]
    kb = lhs.shape[0]
    for j in range(n // IT):
        sl = slice(j * IT, (j + 1) * IT)
        p = jnp.dot(lhs, rhs_ref[:, sl], preferred_element_type=F32)
        m = m_ref[:, sl]
        s = s_ref[:, sl]
        for r in range(0, kb, SUB):
            pr = p[r : r + SUB].reshape(SUB // 8, 8, IT)
            mn = jnp.maximum(m, jnp.max(pr, axis=0))
            e = jnp.sum(jnp.exp2((pr - mn[None]) * k1), axis=0)
            s = s * jnp.exp2((m - mn) * k1) + e
            m = mn
        m_ref[:, sl] = m
        s_ref[:, sl] = s


def m_block(lhs, rhs_ref, x_ref, k1):
    n = rhs_ref.shape[1]
    nacc = None
    ssum = None
    for j in range(n // IT):
        sl = slice(j * IT, (j + 1) * IT)
        p = jnp.dot(lhs, rhs_ref[:, sl], preferred_element_type=F32)
        r = jnp.exp2(p * k1)
        na = r[:, :D] + r[:, D:]
        nacc = na if nacc is None else nacc + na
        sj = jnp.dot(r.astype(BF16), x_ref[sl, :], preferred_element_type=F32)
        ssum = sj if ssum is None else ssum + sj
    cnt = jnp.sum(nacc, axis=1, keepdims=True)
    return ssum / (cnt + COUNT_EPS), cnt


def finish_stats(m_ref, s_ref, k1, out_ref):
    m = m_ref[...]
    top = jnp.max(m, axis=0, keepdims=True)
    tot = jnp.sum(s_ref[...] * jnp.exp2((m - top) * k1), axis=0, keepdims=True)
    out_ref[0:1, :] = top
    out_ref[1:2, :] = tot


def reset_stats(m_ref, s_ref):
    m_ref[...] = jnp.full(m_ref.shape, -jnp.inf, F32)
    s_ref[...] = jnp.zeros(s_ref.shape, F32)


def first_kernel(par_ref, mean_ref, logw_ref, xt_ref, lhs_ref, stat_ref, rhs_ref, m_ref, s_ref):
    step = pl.program_id(0)
    k1, gib, gh, g = par_ref[0, 0], par_ref[0, 1], par_ref[0, 2], par_ref[0, 3]

    @pl.when(step == 0)
    def _():
        reset_stats(m_ref, s_ref)
        fill_rhs(rhs_ref, xt_ref, g, jnp.zeros((1, rhs_ref.shape[1]), F32))

    mu = mean_ref[...]
    sq = jnp.sum(mu * mu, axis=1, keepdims=True)
    c = lane_to_col(logw_ref[...]) * gib - sq * gh
    lhs = jnp.concatenate([mu.astype(BF16), aug_cols(c)], axis=1)
    lhs_ref[...] = lhs
    e_block(lhs, rhs_ref, k1, m_ref, s_ref)

    @pl.when(step == pl.num_programs(0) - 1)
    def _():
        finish_stats(m_ref, s_ref, k1, stat_ref)


def make_mid_kernel(sweep, denom):
    def mid_kernel(par_ref, t_ref, lhs_ref, xt_ref, x_ref, new_ref, stat_ref, rhs_m, rhs_e, m_ref, s_ref):
        step = pl.program_id(0)
        k1 = par_ref[sweep, 0]
        k1n, gib, gh, gn = (par_ref[sweep + 1, i] for i in range(4))

        @pl.when(step == 0)
        def _():
            reset_stats(m_ref, s_ref)
            fill_rhs(rhs_m, xt_ref, par_ref[sweep, 3], t_ref[...])
            fill_rhs(rhs_e, xt_ref, gn, jnp.zeros((1, rhs_e.shape[1]), F32))

        mu, cnt = m_block(lhs_ref[...], rhs_m, x_ref, k1)
        logw = jnp.log((cnt + PRIOR_ALPHA) / denom)
        sq = jnp.sum(mu * mu, axis=1, keepdims=True)
        c = jnp.broadcast_to(logw * gib - sq * gh, mu.shape)
        lhs = jnp.concatenate([mu.astype(BF16), aug_cols(c)], axis=1)
        new_ref[...] = lhs
        e_block(lhs, rhs_e, k1n, m_ref, s_ref)

        @pl.when(step == pl.num_programs(0) - 1)
        def _():
            finish_stats(m_ref, s_ref, k1n, stat_ref)

    return mid_kernel


def make_last_kernel(sweep, denom):
    def last_kernel(par_ref, t_ref, lhs_ref, xt_ref, x_ref, mean_ref, logw_ref, rhs_m):
        k1 = par_ref[sweep, 0]

        @pl.when(pl.program_id(0) == 0)
        def _():
            fill_rhs(rhs_m, xt_ref, par_ref[sweep, 3], t_ref[...])

        mu, cnt = m_block(lhs_ref[...], rhs_m, x_ref, k1)
        mean_ref[...] = mu
        logw_ref[...] = jnp.log((col_to_lane(cnt) + PRIOR_ALPHA) / denom)

    return last_kernel


def solution(mesh):
    row_groups = mesh.shape["pts"]
    comp_groups = mesh.shape["comp"]

    def per_device(points, mean_vecs, log_w, inv_temp):
        n_loc = points.shape[0]
        n = n_loc * row_groups
        k_blk = mean_vecs.shape[0]
        k_total = k_blk * comp_groups
        kl = k_blk // row_groups
        sweeps = inv_temp.shape[0]
        denom = n + k_total * PRIOR_ALPHA
        nb = kl // KB
        p_idx = lax.axis_index("pts")
        x_sq = jnp.einsum("nd,nd->n", points, points, preferred_element_type=F32)
        x = lax.all_gather(points, "pts", tiled=True)
        xt = x.T
        mine = lax.dynamic_slice_in_dim(mean_vecs, p_idx * kl, kl, 0)
        logw = lax.dynamic_slice_in_dim(log_w, p_idx * kl, kl, 0).reshape(kl // D, D)
        g = jnp.where(inv_temp < 2.0**-60, 2.0**-60, jnp.where(inv_temp > 2.0**60, 2.0**60, 1.0)).astype(F32)
        k1 = (inv_temp / g) * (2.0 * LOG2E)
        par = jnp.stack([k1, g / inv_temp * 0.5, g * 0.5, g], axis=1)

        smem = pl.BlockSpec(memory_space=pltpu.SMEM)
        full = lambda s: pl.BlockSpec(s, lambda i: (0, 0))
        blk = lambda w: pl.BlockSpec((KB, w), lambda i: (i, 0))
        lane = pl.BlockSpec((KB // D, D), lambda i: (i, 0))
        rhs = pltpu.VMEM((2 * D, n), BF16)
        acc = pltpu.VMEM((8, n), F32)
        params = pltpu.CompilerParams(vmem_limit_bytes=VMEM)
        unit = 4 * n * kl * D
        lhs_s = jax.ShapeDtypeStruct((kl, 2 * D), BF16)
        stat_s = jax.ShapeDtypeStruct((2, n), F32)

        def cost(k):
            return pl.CostEstimate(flops=k * unit, bytes_accessed=8 * 2**20, transcendentals=n * kl)

        def shift(stat, sweep):
            st = lax.all_gather(stat, ("comp", "pts"))
            top = jnp.max(st[:, 0], axis=0)
            tot = jnp.sum(st[:, 1] * jnp.exp2((st[:, 0] - top) * k1[sweep]), axis=0)
            return (top + jnp.log2(tot) / k1[sweep])[None, :]

        lhs, stat = pl.pallas_call(
            first_kernel, grid=(nb,), name="first",
            out_shape=[lhs_s, stat_s],
            in_specs=[smem, blk(D), lane, full((D, n))],
            out_specs=[blk(2 * D), full((2, n))],
            scratch_shapes=[rhs, acc, acc],
            compiler_params=params, cost_estimate=cost(1),
        )(par, mine, logw, xt)
        for sweep in range(sweeps - 1):
            lhs, stat = pl.pallas_call(
                make_mid_kernel(sweep, denom), grid=(nb,), name="mid",
                out_shape=[lhs_s, stat_s],
                in_specs=[smem, full((1, n)), blk(2 * D), full((D, n)), full((n, D))],
                out_specs=[blk(2 * D), full((2, n))],
                scratch_shapes=[rhs, rhs, acc, acc],
                compiler_params=params, cost_estimate=cost(3),
            )(par, shift(stat, sweep), lhs, xt, x)
        t = shift(stat, sweeps - 1)
        means, logw = pl.pallas_call(
            make_last_kernel(sweeps - 1, denom), grid=(nb,), name="last",
            out_shape=[jax.ShapeDtypeStruct((kl, D), F32), jax.ShapeDtypeStruct((kl // D, D), F32)],
            in_specs=[smem, full((1, n)), blk(2 * D), full((D, n)), full((n, D))],
            out_specs=[blk(D), lane],
            scratch_shapes=[rhs],
            compiler_params=params, cost_estimate=cost(2),
        )(par, t, lhs, xt, x)
        means_out = lax.all_gather(means, "pts", tiled=True)
        logw_out = lax.all_gather(logw, "pts", tiled=True).reshape(k_blk)
        t_mine = lax.dynamic_slice_in_dim(t[0], p_idx * n_loc, n_loc, 0)
        lse = (LN2 * k1[sweeps - 1]) * t_mine - inv_temp[sweeps - 1] * x_sq
        return means_out, logw_out, lse

    row_spec = P(("fit", "pts"))
    comp_spec = P(("fit", "comp"))
    return jax.shard_map(
        per_device,
        mesh=mesh,
        in_specs=(P(("fit", "pts"), None), P(("fit", "comp"), None), comp_spec, P()),
        out_specs=(P(("fit", "comp"), None), comp_spec, row_spec),
        check_vma=False,
    )
```

time: 1280 us -> 316 us (0.25)
  waiting for transfers between devices: 855 us -> 92.2 us
  matrix products: 195 us -> 0 us
  other arithmetic: 183 us -> 9.84 us
  Pallas kernels: 0 us -> 124 us
  blocking collectives: 31.1 us -> 53.8 us
  local copies, waits for them, and re-layouts: 1.43 us -> 20.5 us
    psum x3 -> x0, waiting for transfers between devices: 855 us -> none  [per_device(): counts, stat_sums = lax.psum((counts, stat_sums), 'pts')]
    dot_general x6 -> x0, matrix products: 195 us -> none  [the longest x3 107 us: per_device(): jnp.einsum('nd,kd->nk', points, mean_bf, preferred_element_type=jnp.float32)]
    reduce_sum x9 -> x3, other arithmetic: 162 us -> 2.21 us  [shift(): tot = jnp.sum(st[:, 1] * jnp.exp2((st[:, 0] - top) * k1[sweep]), axis=0)]
    pallas_call x0 -> x4, Pallas kernels: none -> 124 us  [the longest x2 79.8 us: per_device(): pl.pallas_call(make_mid_kernel(sweep, denom), grid=(nb,), name='mid', out...]
    all_gather x0 -> x1, waiting for transfers between devices: none -> 92.2 us  [per_device(): means_out = lax.all_gather(means, 'pts', tiled=True)]
    all_gather x0 -> x5, blocking collectives: none -> 53.8 us  [the longest x3 33.8 us: shift(): st = lax.all_gather(stat, ('comp', 'pts'))]
    div x1 -> x0, other arithmetic: 16.6 us -> none  [per_device(): mean_vecs = stat_sums / (counts[:, None] + COUNT_EPS)]
    pmax x3 -> x0, blocking collectives: 16.1 us -> none  [per_device(): row_top = lax.pmax(jnp.max(logits, axis=1), 'comp')]
  transfers between devices with their start and end apart: 3 -> 1, of which waited for: 3 -> 1; matrix products, arithmetic and copies ran while one was open for 0% -> 1% of each run, Pallas kernels for 0% -> 0%
where the time goes in v1:
time: 316 us; the launch traced here: 315 us
  Pallas kernels  124 us (39%)
  waiting for transfers between devices  92.2 us (29%)
  blocking collectives  53.8 us (17%)
  local copies, waits for them, and re-layouts  20.5 us (6%)
  between operations  14.8 us (5%)
  other arithmetic  9.84 us (3%)
    all_gather x1, waiting for transfers between devices, per_device(): means_out = lax.all_gather(means, 'pts', tiled=True)  92.2 us
    pallas_call x2, Pallas kernels, per_device(): pl.pallas_call(make_mid_kernel(sweep, denom), grid=(nb,), name='mid', out...  79.8 us
    all_gather x3, blocking collectives, shift(): st = lax.all_gather(stat, ('comp', 'pts'))  33.8 us
    pallas_call x1, Pallas kernels, per_device(): pl.pallas_call(make_last_kernel(sweeps - 1, denom), grid=(nb,), name='las...  24.8 us
    pallas_call x1, Pallas kernels, per_device(): pl.pallas_call(first_kernel, grid=(nb,), name='first', out_shape=[lhs_s,...  19.4 us
    unnamed x14, local copies, waits for them, and re-layouts  12.8 us
    all_gather x1, blocking collectives, per_device(): x = lax.all_gather(points, 'pts', tiled=True)  11.9 us
    all_gather x1, blocking collectives, per_device(): logw_out = lax.all_gather(logw, 'pts', tiled=True).reshape(k_blk)  8.09 us
  transfers between devices with their start and end apart: 1, of which 1 were waited for; matrix products, arithmetic and copies ran while one was open for 1% of the time, Pallas kernels for 0%

profile of v1, /device:TPU:0, one launch (start us, length us, event | category | flops | bytes accessed | tf_op | source)
XLA Modules:
  0.0 315.2 jit_solution(16306514572076077307)
XLA Ops:
  7.2 0.0 copy-start
  7.2 0.0 all-gather.8.cloned.1.call-start
  7.2 0.7 divide_multiply_fusion
  7.9 0.1 copy.19
  8.0 0.7 fusion.22
  8.7 0.1 copy.18
  8.8 0.1 copy.17
  8.9 0.1 copy.16
  9.0 11.9 %all_gather.27.x_ref = bf16[2048,128]{1,0:T(8,128)(2,1)S(1)} all-gather(bf16[512,128]{1,0:T(8,128)(2,1)} %param.4), channel_id=1, replica_groups=mesh['fit'=1,'comp'=2,'pts'=4] {'pts'}, dimensions={0}, use_global_device_ids=true | all-gather | bytes 655360 | tf_op jit(solution)/shard_map/all_gather | solution.py:186
  20.8 0.0 copy-start.2
  20.8 1.0 copy.20.xt_ref
  21.8 0.0 copy-done
  21.8 0.6 dynamic-slice_bitcast_fusion.logw_ref
  22.5 4.5 %constant_dynamic-slice_fusion.mean_ref = f32[8192,128]{1,0:T(8,128)} fusion(f32[32768,128]{1,0:T(8,128)} %param.5, s32[]{:T(128)S(6)} %select_n.17), kind=kLoop, calls=%fused_computation.36 | loop fusion | bytes 8388612 | tf_op jit(solution)/shard_map/dynamic_slice | solution.py:188
  26.9 0.0 copy-done.2
  26.9 0.7 pad_maximum_fusion.par_ref
  27.6 19.4 %first.1 = (bf16[8192,256]{1,0:T(8,128)(2,1)}, f32[2,2048]{1,0:T(2,128)}) custom-call(f32[3,4]{1,0:T(4,128)} %pad_maximum_fusion.par_ref, f32[8192,128]{1,0:T(8,128)} %constant_dynamic-slice_fusion.mean_ref, f32[64,128]{1,0:T(8,128)} %dynamic-slice_bitcast_fusion.logw_ref, bf16[128,2048]{1,0:T(8,128)(2,1)} %copy.20.xt_ref), custom_call_target="tpu_custom_call" | custom-call | flops 8589934592 | bytes 8388608 | tf_op jit(solution)/shard_map/first/pallas_call | solution.py:214
  47.0 11.5 %all-gather.3 = f32[8,2,2048]{2,1,0:T(2,128)S(1)} all-gather(f32[1,2,2048]{2,1,0:T(2,128)} %bitcast.75), channel_id=2, replica_groups=mesh['fit'=1,'comp'=2,'pts'=4] {'comp','pts'}, dimensions={0}, use_global_device_ids=true | all-gather | bytes 147456 | tf_op jit(solution)/shard_map/all_gather | solution.py:209
  58.5 0.1 fusion.21
  58.6 0.8 fusion.14
  59.3 1.3 divide_add_fusion.2
  60.6 39.9 %mid.2 = (bf16[8192,256]{1,0:T(8,128)(2,1)}, f32[2,2048]{1,0:T(2,128)}) custom-call(f32[3,4]{1,0:T(4,128)} %pad_maximum_fusion.par_ref, f32[1,2048]{1,0:T(1,128)} %bitcast.80, bf16[8192,256]{1,0:T(8,128)(2,1)} %get-tuple-element.12.lhs_ref, bf16[128,2048]{1,0:T(8,128)(2,1)} %copy.20.xt_ref, bf16[2048,128]{1,0:T(8,128)(2,1)} %copy-done.2), custom_call_target="tpu_custom_call" | custom-call | flops 25769803776 | bytes 8388608 | tf_op jit(solution)/shard_map/mid/pallas_call | solution.py:223
  100.5 11.3 %all-gather.4 = f32[8,2,2048]{2,1,0:T(2,128)S(1)} all-gather(f32[1,2,2048]{2,1,0:T(2,128)} %bitcast.76), channel_id=3, replica_groups=mesh['fit'=1,'comp'=2,'pts'=4] {'comp','pts'}, dimensions={0}, use_global_device_ids=true | all-gather | bytes 147456 | tf_op jit(solution)/shard_map/all_gather | solution.py:209
  111.8 0.1 fusion.20
  111.9 0.7 fusion.8
  112.6 1.2 divide_add_fusion.1
  113.9 39.9 %mid.3 = (bf16[8192,256]{1,0:T(8,128)(2,1)}, f32[2,2048]{1,0:T(2,128)}) custom-call(f32[3,4]{1,0:T(4,128)} %pad_maximum_fusion.par_ref, f32[1,2048]{1,0:T(1,128)} %bitcast.81, bf16[8192,256]{1,0:T(8,128)(2,1)} %get-tuple-element.14.lhs_ref, bf16[128,2048]{1,0:T(8,128)(2,1)} %copy.20.xt_ref, bf16[2048,128]{1,0:T(8,128)(2,1)} %copy-done.2), custom_call_target="tpu_custom_call" | custom-call | flops 25769803776 | bytes 8388608 | tf_op jit(solution)/shard_map/mid/pallas_call | solution.py:223
  153.8 11.1 %all-gather.5 = f32[8,2,2048]{2,1,0:T(2,128)S(1)} all-gather(f32[1,2,2048]{2,1,0:T(2,128)} %bitcast.77), channel_id=4, replica_groups=mesh['fit'=1,'comp'=2,'pts'=4] {'comp','pts'}, dimensions={0}, use_global_device_ids=true | all-gather | bytes 147456 | tf_op jit(solution)/shard_map/all_gather | solution.py:209
  164.9 0.1 fusion.19
  165.0 0.8 fusion.2
  165.8 1.3 divide_add_fusion
  167.1 24.8 %last.1 = (f32[8192,128]{1,0:T(8,128)}, f32[64,128]{1,0:T(8,128)}) custom-call(f32[3,4]{1,0:T(4,128)} %pad_maximum_fusion.par_ref, f32[1,2048]{1,0:T(1,128)} %bitcast.78, bf16[8192,256]{1,0:T(8,128)(2,1)} %get-tuple-element.16.lhs_ref, bf16[128,2048]{1,0:T(8,128)(2,1)} %copy.20.xt_ref, bf16[2048,128]{1,0:T(8,128)(2,1)} %copy-done.2), custom_call_target="tpu_custom_call" | custom-call | flops 17179869184 | bytes 8388608 | tf_op jit(solution)/shard_map/last/pallas_call | solution.py:232
  191.8 0.0 copy-start.5
  191.8 0.0 copy-start.4
  191.8 0.0 copy-start.3
  191.9 0.0 all-gather.8.cloned.1.call-update
  191.9 0.6 copy-done.5
  192.5 0.6 slice.46
  193.8 0.0 copy-done.4
  193.8 8.1 %all_gather.35 = f32[256,128]{1,0:T(8,128)S(1)} all-gather(f32[64,128]{1,0:T(8,128)S(1)} %copy-done.4), channel_id=1, replica_groups=mesh['fit'=1,'comp'=2,'pts'=4] {'pts'}, dimensions={0}, use_global_device_ids=true | all-gather | bytes 163840 | tf_op jit(solution)/shard_map/all_gather | solution.py:241
  201.9 0.0 copy-done.3
  201.9 0.1 fusion
  202.1 1.9 multiply_subtract_fusion
  204.0 92.2 %all-gather.8.cloned.1.call-done = f32[32768,128]{1,0:T(8,128)} async-done(((f32[8192,128]{1,0:T(8,128)}), f32[32768,128]{1,0:T(8,128)}) %all-gather.8.cloned.1.call-update) | async-done | bytes 16777232 | tf_op jit(solution)/shard_map/all_gather | solution.py:240
  296.2 0.0 copy-start.1
  296.2 11.5 %copy.81 = f32[32768,128]{1,0:T(8,128)} copy(f32[32768,128]{1,0:T(8,128)} %all-gather.8.cloned.1.call-done) | data formatting | bytes 33554432
  307.7 0.7 copy.82
  308.4 0.0 copy-done.1
Async XLA Ops:
  7.2 14.7 %copy-start = (f32[32768]{0:T(1024)S(1)}, f32[32768]{0:T(1024)}, u32[]{:S(2)}) copy-start(f32[32768]{0:T(1024)} %param.6) | copy-start | bytes 393220
  7.2 289.0 %all-gather.8.cloned.1.call-start = ((), (), s32[]{:S(2)}) async-start(), calls=%async_computation | async-start | bytes 20971520 | tf_op jit(solution)/shard_map/all_gather | solution.py:240
  20.8 6.1 %copy-start.2 = (bf16[2048,128]{1,0:T(8,128)(2,1)}, bf16[2048,128]{1,0:T(8,128)(2,1)S(1)}, u32[]{:S(2)}) copy-start(bf16[2048,128]{1,0:T(8,128)(2,1)S(1)} %all_gather.27.x_ref) | copy-start | bytes 1572868
  191.8 0.7 copy-start.5
  191.8 2.0 copy-start.4
  191.8 10.1 %copy-start.3 = (bf16[512,128]{1,0:T(8,128)(2,1)S(1)}, bf16[512,128]{1,0:T(8,128)(2,1)}, u32[]{:S(2)}) copy-start(bf16[512,128]{1,0:T(8,128)(2,1)} %param.4) | copy-start | bytes 393220
  296.2 12.1 %copy-start.1 = (f32[32768]{0:T(1024)S(1)}, f32[32768]{0:T(1024)}, u32[]{:S(2)}) copy-start(f32[32768]{0:T(1024)} %param.6) | copy-start | bytes 393220
Sparse Core Ops, SparseCore 0:
  192.0 104.1 all-gather.7

commit v2 on v0

v2 whole, which is shorter than its diff:
```python
import jax
import jax.numpy as jnp
from jax import lax
from jax.experimental import pallas as pl
from jax.experimental.pallas import tpu as pltpu
from jax.sharding import PartitionSpec as P

PRIOR_ALPHA = 1e-3
COUNT_EPS = 1e-6
LOG2E = 1.4426950408889634
LN2 = 0.6931471805599453
F32 = jnp.float32
BF16 = jnp.bfloat16
D = 128
KB = 1024
IT = 256
SUB = 64
VMEM = 46 * 2**20
NPTS = 4
NDEV = 8
MESH = pl.DeviceIdType.MESH
FAR = 6
EARLY = 5


def split3(v):
    hi = v.astype(BF16).astype(F32)
    mid = (v - hi).astype(BF16).astype(F32)
    return hi, mid, v - hi - mid


def lane_to_col(rows):
    r = rows.shape[0]
    eye = lax.broadcasted_iota(jnp.int32, (1, D, D), 1) == lax.broadcasted_iota(jnp.int32, (1, D, D), 2)
    col = jnp.sum(jnp.where(eye, rows[:, None, :], 0.0), axis=2, keepdims=True)
    return jnp.broadcast_to(col, (r, D, D)).reshape(r * D, D)


def col_to_lane(col):
    r = col.shape[0] // D
    eye = lax.broadcasted_iota(jnp.int32, (1, D, D), 1) == lax.broadcasted_iota(jnp.int32, (1, D, D), 2)
    return jnp.sum(jnp.where(eye, jnp.broadcast_to(col, (r * D, D)).reshape(r, D, D), 0.0), axis=1)


def aug_cols(c):
    lane = lax.broadcasted_iota(jnp.int32, c.shape, 1)
    hi, mid, lo = split3(c)
    v = jnp.where(lane == 0, hi, jnp.where(lane == 1, mid, lo))
    v = jnp.where(lane < 3, v, jnp.where(lane < 6, 1.0, 0.0))
    return v.astype(BF16)


def aug_rows(t):
    row = lax.broadcasted_iota(jnp.int32, (D, t.shape[1]), 0)
    hi, mid, lo = split3(-t)
    v = jnp.where(row == 3, hi, jnp.where(row == 4, mid, lo))
    v = jnp.where(row < 3, 1.0, jnp.where(row < 6, v, 0.0))
    return v.astype(BF16)


def fill_rhs(rhs_ref, xt_ref, g, t):
    rhs_ref[0:D, :] = (xt_ref[...].astype(F32) * g).astype(BF16)
    rhs_ref[D:, :] = aug_rows(t)


def m_part(lhs, rhs_ref, x_ref, k1, j, nacc, ssum):
    sl = slice(j * IT, (j + 1) * IT)
    r = jnp.exp2(jnp.dot(lhs, rhs_ref[:, sl], preferred_element_type=F32) * k1)
    na = r[:, :D] + r[:, D:]
    sj = jnp.dot(r.astype(BF16), x_ref[sl, :], preferred_element_type=F32)
    return (na, sj) if nacc is None else (nacc + na, ssum + sj)


def m_block(lhs, rhs_ref, x_ref, k1):
    nacc = ssum = None
    for j in range(rhs_ref.shape[1] // IT):
        nacc, ssum = m_part(lhs, rhs_ref, x_ref, k1, j, nacc, ssum)
    return nacc, ssum


def e_part(lhs, rhs_ref, k1, j, m_ref, s_ref):
    sl = slice(j * IT, (j + 1) * IT)
    kb = lhs.shape[0]
    p = jnp.dot(lhs, rhs_ref[:, sl], preferred_element_type=F32)
    m = m_ref[:, sl]
    s = s_ref[:, sl]
    for r in range(0, kb, SUB):
        pr = p[r : r + SUB].reshape(SUB // 8, 8, IT)
        mn = jnp.maximum(m, jnp.max(pr, axis=0))
        e = jnp.sum(jnp.exp2((pr - mn[None]) * k1), axis=0)
        s = s * jnp.exp2((m - mn) * k1) + e
        m = mn
    m_ref[:, sl] = m
    s_ref[:, sl] = s


def reset_stats(m_ref, s_ref):
    m_ref[...] = jnp.full(m_ref.shape, -jnp.inf, F32)
    s_ref[...] = jnp.zeros(s_ref.shape, F32)


def make_kernel(denom, sweeps):
    def kernel(par_ref, pts_ref, mean_ref, logw_ref, out_ref, lw_out, lse_out,
               x_ref, xt_ref, rhs_m, rhs_e, a_ref, b_ref, mean_s, logw_s, mu_send, c_send, mu_far, c_far,
               m_ref, s_ref, s_s, n_s, aug, stat, gat,
               in_sem, xs, xr, ss, sr, bs, br, cs, cr, ds, dr, fs, fr, ws, wr, ls, lr):
        c = lax.axis_index("comp")
        p = lax.axis_index("pts")
        rows = pts_ref.shape[0]
        n = x_ref.shape[0]
        kl = b_ref.shape[0]
        nb = kl // KB
        nj = n // IT
        lb = KB // D
        q_far = lax.rem(p + 2, NPTS)
        q_sib = p + 1 - 2 * lax.rem(p, 2)
        q_dia = lax.rem(q_sib + 2, NPTS)
        sib, opp = {"pts": q_sib}, {"pts": q_far}
        me = c * NPTS + p
        others = []
        for off in range(1, NDEV):
            pos = lax.rem(me + off, NDEV)
            others.append((off, {"comp": pos // NPTS, "pts": lax.rem(pos, NPTS)}))

        def blk(base, i, size=KB):
            return pl.ds(pl.multiple_of(base + i * size, size), size)

        def remote(src, dst, send, recv, dev):
            return pltpu.make_async_remote_copy(src_ref=src, dst_ref=dst, send_sem=send, recv_sem=recv,
                                                device_id=dev, device_id_type=MESH)

        loads = [pltpu.make_async_copy(mean_ref.at[blk(p * kl, i)], mean_s.at[pl.ds(i * KB, KB)], in_sem.at[i])
                 for i in range(nb)]
        loads.append(pltpu.make_async_copy(logw_ref.at[blk(0, p, kl // D)], logw_s, in_sem.at[nb]))
        for cp in loads:
            cp.start()
        barrier = pltpu.get_barrier_semaphore()
        for _, dev in others:
            pl.semaphore_signal(barrier, inc=1, device_id=dev, device_id_type=MESH)
        pl.semaphore_wait(barrier, NDEV - 1)

        mine = blk(0, p, rows)
        xsend = [remote(pts_ref, x_ref.at[mine], xs.at[off], xr.at[off], {"pts": lax.rem(p + off, NPTS)})
                 for off in range(1, NPTS)]
        for cp in xsend:
            cp.start()
        x_ref[mine, :] = pts_ref[...]

        k1, gib, gh, g = (par_ref[0, i] for i in range(4))
        loads[nb].wait()

        def prep(i, carry):
            pltpu.make_async_copy(mean_ref.at[blk(p * kl, i)], mean_s.at[blk(0, i)], in_sem.at[i]).wait()
            mu = mean_s[blk(0, i), :]
            sq = jnp.sum(mu * mu, axis=1, keepdims=True)
            cc = lane_to_col(logw_s[blk(0, i, lb), :]) * gib - sq * gh
            a_ref[blk(0, i), :] = jnp.concatenate([mu.astype(BF16), aug_cols(cc)], axis=1)
            return carry

        lax.fori_loop(0, nb, prep, 0)
        for cp in xsend:
            cp.wait()
        xt_ref[...] = x_ref[...].astype(F32).T.astype(BF16)

        def exchange(rnd, k1, between=None):
            m = m_ref[...]
            top = jnp.max(m, axis=0, keepdims=True)
            stat[rnd, 0:1, :] = top
            stat[rnd, 1:2, :] = jnp.sum(s_ref[...] * jnp.exp2((m - top) * k1), axis=0, keepdims=True)
            sends = [remote(stat.at[rnd], gat.at[rnd, off], ss.at[rnd, off], sr.at[rnd, off], dev) for off, dev in others]
            for cp in sends:
                cp.start()
            if between is not None:
                between()
            for cp in sends:
                cp.wait()
            top = stat[rnd, 0:1, :]
            for off in range(1, NDEV):
                top = jnp.maximum(top, gat[rnd, off, 0:1, :])
            tot = stat[rnd, 1:2, :] * jnp.exp2((stat[rnd, 0:1, :] - top) * k1)
            for off in range(1, NDEV):
                tot += gat[rnd, off, 1:2, :] * jnp.exp2((gat[rnd, off, 0:1, :] - top) * k1)
            return top + jnp.log2(tot) / k1

        reset_stats(m_ref, s_ref)
        fill_rhs(rhs_e, xt_ref, g, jnp.zeros((1, n), F32))

        def e_step(i, carry):
            lhs = a_ref[blk(0, i), :]
            for j in range(nj):
                e_part(lhs, rhs_e, k1, j, m_ref, s_ref)
            return carry

        lax.fori_loop(0, nb, e_step, 0)
        t = exchange(0, k1)

        def bulk(i):
            return (remote(mu_send.at[blk(0, i)], mu_far.at[blk(0, i)], bs.at[i], br.at[i], opp),
                    remote(c_send.at[blk(0, i, lb)], c_far.at[blk(0, i, lb)], cs.at[i], cr.at[i], opp))

        for sweep in range(sweeps - 1):
            src, dst = (a_ref, b_ref) if sweep % 2 == 0 else (b_ref, a_ref)
            share = sweep == sweeps - 2
            k1 = par_ref[sweep, 0]
            k1n, gib, gh, gn = (par_ref[sweep + 1, i] for i in range(4))
            fill_rhs(rhs_m, xt_ref, par_ref[sweep, 3], t)
            fill_rhs(rhs_e, xt_ref, gn, jnp.zeros((1, n), F32))
            reset_stats(m_ref, s_ref)

            def epilogue(i, dst=dst, share=share, gib=gib, gh=gh):
                cnt = jnp.sum(n_s[...], axis=1, keepdims=True)
                mu = s_s[...] / (cnt + COUNT_EPS)
                logw = jnp.log((cnt + PRIOR_ALPHA) / denom)
                sq = jnp.sum(mu * mu, axis=1, keepdims=True)
                cc = jnp.broadcast_to(logw * gib - sq * gh, mu.shape)
                mu_bf = mu.astype(BF16)
                aug[...] = jnp.concatenate([mu_bf, aug_cols(cc)], axis=1)
                dst[blk(0, i), :] = aug[...]
                if share:
                    mu_send[blk(0, i), :] = mu_bf
                    c_send[blk(0, i, lb), :] = col_to_lane(cc)

            n_s[...], s_s[...] = m_block(src[0:KB, :], rhs_m, x_ref, k1)

            def mid_step(i, carry, src=src, share=share, k1=k1, k1n=k1n, epilogue=epilogue):
                lhs = src[blk(0, i), :]
                nacc, ssum = m_part(lhs, rhs_m, x_ref, k1, 0, None, None)
                epilogue(i - 1)
                for j in range(1, nj):
                    nacc, ssum = m_part(lhs, rhs_m, x_ref, k1, j, nacc, ssum)
                    e_part(aug[...], rhs_e, k1n, j - 1, m_ref, s_ref)
                e_part(aug[...], rhs_e, k1n, nj - 1, m_ref, s_ref)
                n_s[...] = nacc
                s_s[...] = ssum
                if share:
                    @pl.when(i - 1 < EARLY)
                    def _():
                        for cp in bulk(i - 1):
                            cp.start()
                return carry

            lax.fori_loop(1, nb, mid_step, 0)
            epilogue(nb - 1)
            for j in range(nj):
                e_part(aug[...], rhs_e, k1n, j, m_ref, s_ref)

            def rest():
                for i in range(EARLY, FAR):
                    for cp in bulk(i):
                        cp.start()

            t = exchange(sweep + 1, k1n, rest if share else None)

        k1, beta, g = par_ref[sweeps - 1, 0], par_ref[sweeps - 1, 4], par_ref[sweeps - 1, 3]
        fill_rhs(rhs_m, xt_ref, g, t)
        stat[0, 0:1, :] = t
        own = pl.ds(pl.multiple_of(p * rows, rows), rows)
        xo = xt_ref[:, own].astype(F32)
        lse_out[...] = (LN2 * k1) * stat[0, 0:1, own] - beta * jnp.sum(xo * xo, axis=0, keepdims=True)

        late = nb - FAR

        def place(i, near_q, far_q):
            near = lax.rem(i + FAR, nb)
            return jnp.where(i < nb, near_q * nb + near, far_q * nb + i - nb)

        def to_sib(i, own_side=True):
            pos = place(i, p, q_far) if own_side else place(i, q_sib, q_dia)
            return remote(out_ref.at[blk(0, pos)], out_ref.at[blk(0, pos)], ds.at[i], dr.at[i], sib)

        def to_opp(i, q=None):
            rows_ = out_ref.at[blk(0, (p if q is None else q) * nb + FAR + i)]
            return remote(rows_, rows_, fs.at[i], fr.at[i], opp)

        def forward(i, q=None):
            rows_ = out_ref.at[blk(0, (q_far if q is None else q) * nb + FAR + i)]
            return remote(rows_, rows_, ws.at[i], wr.at[i], sib)

        def lw(k, q, first, count, dev):
            r_ = lw_out.at[pl.ds(pl.multiple_of((q * nb + first) * lb, lb), count * lb)]
            return remote(r_, r_, ls.at[k], lr.at[k], dev)

        def last_step(i, carry):
            pos_l = jnp.where(i < nb, lax.rem(i + FAR, nb), i)
            pos = place(i, p, q_far)
            nacc, ssum = m_block(a_ref[blk(0, pos_l), :], rhs_m, x_ref, k1)
            cnt = jnp.sum(nacc, axis=1, keepdims=True)
            out_ref[blk(0, pos), :] = ssum / (cnt + COUNT_EPS)
            lw_out[blk(0, pos, lb), :] = jnp.log((col_to_lane(cnt) + PRIOR_ALPHA) / denom)

            @pl.when(i < FAR)
            def _():
                for cp in bulk(i):
                    cp.wait()
                a_ref[blk(kl, i), :] = jnp.concatenate(
                    [mu_far[blk(0, i), :], aug_cols(lane_to_col(c_far[blk(0, i, lb), :]))], axis=1)

            to_sib(i).start()

            @pl.when(i < late)
            def _():
                to_opp(i).start()

            @pl.when(i == late)
            def _():
                lw(0, p, FAR, late, opp).start()

            @pl.when(i == nb)
            def _():
                lw(1, p, 0, nb, sib).start()

            for k in range(late):
                @pl.when(i == nb + FAR - 2 * (late - k))
                def _(k=k):
                    to_opp(k, q_far).wait_recv()
                    forward(k).start()
            return carry

        steps = nb + FAR
        lax.fori_loop(0, steps, last_step, 0)
        lw(2, q_far, 0, FAR, sib).start()
        lw(0, q_far, FAR, late, opp).wait_recv()
        lw(3, q_far, FAR, late, sib).start()

        def drain(i, carry):
            to_sib(i).wait_send()
            to_sib(i, False).wait_recv()
            return carry

        lax.fori_loop(0, steps, drain, 0)
        for k in range(late):
            to_opp(k).wait_send()
            forward(k).wait_send()
            forward(k, q_dia).wait_recv()
        lw(0, p, FAR, late, opp).wait_send()
        lw(1, p, 0, nb, sib).wait_send()
        lw(1, q_sib, 0, nb, sib).wait_recv()
        lw(2, q_far, 0, FAR, sib).wait_send()
        lw(2, q_dia, 0, FAR, sib).wait_recv()
        lw(3, q_far, FAR, late, sib).wait_send()
        lw(3, q_dia, FAR, late, sib).wait_recv()

    return kernel


def solution(mesh):
    row_groups = mesh.shape["pts"]
    comp_groups = mesh.shape["comp"]

    def per_device(points, mean_vecs, log_w, inv_temp):
        n_loc = points.shape[0]
        n = n_loc * row_groups
        k_blk = mean_vecs.shape[0]
        k_total = k_blk * comp_groups
        kl = k_blk // row_groups
        nb = kl // KB
        late = nb - FAR
        sweeps = inv_temp.shape[0]
        denom = n + k_total * PRIOR_ALPHA
        g = jnp.where(inv_temp < 2.0**-60, 2.0**-60, jnp.where(inv_temp > 2.0**60, 2.0**60, 1.0)).astype(F32)
        k1 = (inv_temp / g) * (2.0 * LOG2E)
        par = jnp.stack([k1, g / inv_temp * 0.5, g * 0.5, g, inv_temp], axis=1)
        vm = pltpu.VMEM
        dma = lambda *s: pltpu.SemaphoreType.DMA(s)
        anyspace = pl.BlockSpec(memory_space=pl.ANY)
        vspec = pl.BlockSpec(memory_space=pltpu.VMEM)
        means, logw, lse = pl.pallas_call(
            make_kernel(denom, sweeps), name="em",
            out_shape=[vm((k_blk, D), F32), vm((k_blk // D, D), F32), vm((1, n_loc), F32)],
            in_specs=[pl.BlockSpec(memory_space=pltpu.SMEM), vspec, anyspace, anyspace],
            out_specs=[vspec, vspec, vspec],
            scratch_shapes=[
                vm((n, D), BF16), vm((D, n), BF16), vm((2 * D, n), BF16), vm((2 * D, n), BF16),
                vm((kl + FAR * KB, 2 * D), BF16), vm((kl, 2 * D), BF16), vm((kl, D), F32), vm((kl // D, D), F32),
                vm((kl, D), BF16), vm((kl // D, D), F32), vm((FAR * KB, D), BF16), vm((FAR * KB // D, D), F32),
                vm((8, n), F32), vm((8, n), F32), vm((KB, D), F32), vm((KB, D), F32), vm((KB, 2 * D), BF16),
                vm((sweeps, 2, n), F32), vm((sweeps, NDEV, 2, n), F32),
                dma(nb + 1), dma(NPTS), dma(NPTS), dma(sweeps, NDEV), dma(sweeps, NDEV),
                dma(FAR), dma(FAR), dma(FAR), dma(FAR), dma(nb + FAR), dma(nb + FAR), dma(late), dma(late),
                dma(late), dma(late), dma(4), dma(4)],
            compiler_params=pltpu.CompilerParams(collective_id=0, has_side_effects=True, vmem_limit_bytes=VMEM),
        )(par, points, mean_vecs, log_w.reshape(k_blk // D, D))
        return means, logw.reshape(k_blk), lse.reshape(n_loc)

    row_spec = P(("fit", "pts"))
    comp_spec = P(("fit", "comp"))
    return jax.shard_map(
        per_device,
        mesh=mesh,
        in_specs=(P(("fit", "pts"), None), P(("fit", "comp"), None), comp_spec, P()),
        out_specs=(P(("fit", "comp"), None), comp_spec, row_spec),
        check_vma=False,
    )
```

time: 1280 us -> 160 us (0.12)
  waiting for transfers between devices: 855 us -> 0 us
  matrix products: 195 us -> 0 us
  other arithmetic: 183 us -> 0.66 us
  Pallas kernels: 0 us -> 149 us
  blocking collectives: 31.1 us -> 0 us
  between operations: 13.8 us -> 0.64 us
    psum x3 -> x0, waiting for transfers between devices: 855 us -> none  [per_device(): counts, stat_sums = lax.psum((counts, stat_sums), 'pts')]
    dot_general x6 -> x0, matrix products: 195 us -> none  [the longest x3 107 us: per_device(): jnp.einsum('nd,kd->nk', points, mean_bf, preferred_element_type=jnp.float32)]
    reduce_sum x9 -> x0, other arithmetic: 162 us -> none  [the longest x3 66.9 us: per_device(): counts = jnp.sum(resp_prob, axis=0)]
    pallas_call x0 -> x1, Pallas kernels: none -> 149 us  [per_device(): pl.pallas_call(make_kernel(denom, sweeps), name='em', out_shape=[vm((k_bl...]
    div x1 -> x0, other arithmetic: 16.6 us -> none  [per_device(): mean_vecs = stat_sums / (counts[:, None] + COUNT_EPS)]
    pmax x3 -> x0, blocking collectives: 16.1 us -> none  [per_device(): row_top = lax.pmax(jnp.max(logits, axis=1), 'comp')]
    psum x3 -> x0, blocking collectives: 15 us -> none  [per_device(): lax.psum(jnp.sum(jnp.exp(logits - row_top[:, None]), axis=1), 'comp')]
  transfers between devices with their start and end apart: 3 -> 0, of which waited for: 3 -> 0; matrix products, arithmetic and copies ran while one was open for 0% -> 0% of each run, Pallas kernels for 0% -> 0%
where the time goes in v2:
time: 160 us
  Pallas kernels  149 us (93%)
  local copies, waits for them, and re-layouts  9.19 us (6%)
    pallas_call x1, Pallas kernels, per_device(): pl.pallas_call(make_kernel(denom, sweeps), name='em', out_shape=[vm((k_bl...  149 us
    unnamed x3, local copies, waits for them, and re-layouts  7.41 us

profile of v2, /device:TPU:0, one launch (start us, length us, event | category | flops | bytes accessed | tf_op | source)
XLA Modules:
  0.0 159.8 jit_solution(2675435886369111468)
XLA Ops:
  0.6 0.7 copy.11
  1.4 0.7 fusion
  2.0 0.1 copy.10
  2.1 0.1 copy.7
  2.2 0.1 copy.9
  2.3 0.1 copy.8
  2.4 0.7 stack.23.par_ref
  3.1 149.4 %em.1 = (f32[32768,128]{1,0:T(8,128)S(1)}, f32[256,128]{1,0:T(8,128)S(1)}, f32[1,512]{1,0:T(1,128)S(1)}) custom-call(f32[3,5]{1,0:T(4,128)} %stack.23.par_ref, bf16[512,128]{1,0:T(8,128)(2,1)} %pts_ref.1, f32[32768,128]{1,0:T(8,128)} %mean_ref.1, f32[256,128]{1,0:T(8,128)} %bitcast.14), custom_call_target="tpu_custom_call" | custom-call | tf_op jit(solution)/shard_map/em/pallas_call | solution.py:367
  152.4 6.2 %copy.15 = f32[32768,128]{1,0:T(8,128)} copy(f32[32768,128]{1,0:T(8,128)S(1)} %get-tuple-element.13) | data formatting | bytes 33554432
  158.6 0.7 copy.16
  159.3 0.6 copy.17
